TPU v7x, 32 devices: a whole 2x2x4 slice. The times are simulated.
32 devices in a mesh: tm: 4 (over y, x), lat: 8 (over z, core).
Axes of the slice: x: 2, y: 2, z: 4, core: 2. Of those that a mesh axis runs over, the one named last changes fastest.
Arguments:
- sketch: bfloat16 [256, 3, 64, 1024], P('tm', None, 'lat'), may hold values from -6 to 6
- test_sketch: bfloat16 [256, 3, 64, 1024], P('tm', None, 'lat'), may hold values from -6 to 6
- checkpoints: bfloat16 [16, 3, 64, 1024], P('tm', None, 'lat'), may hold values from -2.5 to 2.5
- checkpoint_step: int32 [4], P('tm'), may hold values from 0 to 3
- station_row: int32 [4, 1024], P('tm', 'lat'), may hold values from 0 to 63, as said below
- station_column: int32 [4, 1024], P('tm', 'lat'), may hold values from 0 to 1023
- station_value: float32 [4, 1024], P('tm', 'lat'), may hold values from -6 to 6
Outputs:
- increment: float32 [4, 3, 64, 1024], P('tm', None, 'lat')
- reduced_adjoint: float32 [4, 64], P('tm')
- total_cost: float32 [], replicated
Inputs may be any that keep to these rules, and one draw needn't show every extreme that they name: `station_row`: in each group's list, entries 128 * j to 128 * (j + 1) - 1 lie in latitude rows 8 * j to 8 * (j + 1) - 1.
All inputs are finite; a program needn't handle non-finite values.
Results may differ from a plain program's by a relative error of at most 0.0003.
Values may be sent and summed in bfloat16 or wider, within the bound.
A program may use at most 128 MiB of HBM per device.

v0:
```python
import functools
import math

import jax
import jax.numpy as jnp
from jax import lax
from jax.experimental import pallas as pl
from jax.experimental.pallas import tpu as pltpu
from jax.sharding import PartitionSpec as P

STEPS = 4
LANES = 128

wave_coef = 0.5
flow_coef = 0.4
coriolis_coef = 0.5
map_scale = 0.5

MESH = pl.DeviceIdType.MESH


def dlat(field):
    count = field.shape[0]
    return pltpu.roll(field, count - 1, 0) - pltpu.roll(field, 1, 0)


def advance(state, coefs, turn, dlon):
    half = 0.5 * wave_coef
    dx_height, dx_east, dx_north = (dlon(values) for values in state)
    out = [], [], []
    for tile, (height, east, north) in enumerate(zip(*state)):
        depth, east_flow, north_flow = (values[tile] for values in coefs)
        dy_north = dlat(north)
        dy_height = dlat(height)
        out[0].append(
            height
            - depth * (dx_east[tile] + dy_north)
            - (east_flow * dx_height[tile] + north_flow * dy_height)
        )
        out[1].append(
            east
            + turn * north
            - half * dx_height[tile]
            - (east_flow * dx_east[tile] + north_flow * dlat(east))
        )
        out[2].append(
            north
            - turn * east
            - half * dy_height
            - (east_flow * dx_north[tile] + north_flow * dy_north)
        )
    return enumerate(out)


def advance_adjoint(state, coefs, turn, dlon):
    half = 0.5 * wave_coef
    heights, easts, norths = state
    depths, east_flows, north_flows = coefs
    cells = list(zip(heights, easts, norths, depths, east_flows, north_flows))
    dx = dlon([half * u + e * h for h, u, v, d, e, n in cells])
    yield 0, [h + x + dlat(half * v + n * h) for x, (h, u, v, d, e, n) in zip(dx, cells)]
    dx = dlon([d * h + e * u for h, u, v, d, e, n in cells])
    yield 1, [u - turn * v + x + dlat(n * u) for x, (h, u, v, d, e, n) in zip(dx, cells)]
    dx = dlon([e * v for h, u, v, d, e, n in cells])
    yield 2, [v + turn * u + x + dlat(d * h + n * v) for x, (h, u, v, d, e, n) in zip(dx, cells)]


def kernel(
    groups,
    bands,
    sketch_hbm,
    test_hbm,
    stored_hbm,
    chosen,
    row_hbm,
    column_hbm,
    value_hbm,
    increment,
    adjoint,
    total_cost,
    sketch,
    test,
    beyond,
    sketch_wide,
    test_wide,
    beyond_wide,
    stored,
    station_row,
    station_column,
    station_value,
    coef_ext,
    ext,
    spare,
    forced,
    forced_beyond,
    folded,
    spread,
    base_send,
    base_recv,
    field_send,
    field_recv,
    last_send,
    last_recv,
    message,
    later_in,
    own_in,
    cost_out,
    cost_in,
    cost_group_out,
    cost_group_in,
    cost_here,
    load_sem,
    beyond_ss,
    beyond_rs,
    base_ss,
    base_rs,
    field_ss,
    field_rs,
    last_ss,
    last_rs,
    later_ss,
    later_rs,
    own_ss,
    own_rs,
    cost_ss,
    cost_rs,
    cost_group_ss,
    cost_group_rs,
):
    rank, fields, rows, columns = sketch.shape
    halo = STEPS
    group = lax.axis_index("tm")
    band = lax.axis_index("lat")
    total_rows = rows * bands
    observed = station_row.shape[1] * bands
    tiles = columns // LANES

    loads = [
        pltpu.make_async_copy(source, target, load_sem.at[index])
        for index, (source, target) in enumerate(
            (
                (row_hbm, station_row),
                (column_hbm, station_column),
                (value_hbm, station_value),
                (stored_hbm, stored),
                (sketch_hbm.at[:, :1], sketch.at[:, :1]),
                (sketch_hbm.at[:, 1:], sketch.at[:, 1:]),
                (test_hbm, test),
            )
        )
    ]
    for load in loads[:6]:
        load.start()

    barrier = pltpu.get_barrier_semaphore()
    last_group = groups - 1

    def each(count, first, action):
        for index in range(first, count):
            action(index)

    def greet(place):
        pl.semaphore_signal(barrier, inc=1, device_id=place, device_id_type=MESH)

    @pl.when(group < last_group)
    def _():
        each(bands, 0, lambda index: greet({"tm": group + 1, "lat": index}))

    each(bands, 1, lambda offset: greet({"lat": lax.rem(band + offset, bands)}))

    for offset in range(2, groups):

        @pl.when(group + offset < groups)
        def _():
            greet({"tm": group + offset})

    for offset in range(1, groups):

        @pl.when(group - offset >= 0)
        def _():
            greet({"tm": group - offset})

    later = jnp.minimum(group, 1)
    greetings = bands - 1 + groups - 1 + (bands - 1) * later

    def remote(source, target, send_sem, recv_sem, where):
        return pltpu.make_async_remote_copy(
            src_ref=source,
            dst_ref=target,
            send_sem=send_sem,
            recv_sem=recv_sem,
            device_id=where,
            device_id_type=MESH,
        )

    below = {"lat": jnp.maximum(band - 1, 0)}
    above = {"lat": jnp.minimum(band + 1, bands - 1)}

    def halo_copies(send, recv, ss, rs, field):
        down = remote(
            send.at[0, field], recv.at[1, field], ss.at[0, field], rs.at[1, field], below
        )
        up = remote(send.at[1, field], recv.at[0, field], ss.at[1, field], rs.at[0, field], above)
        return down, up

    def halo_start(exchange, field):
        recv = exchange[1]
        down, up = halo_copies(*exchange, field)

        @pl.when(band > 0)
        def _():
            down.start()

        @pl.when(band == 0)
        def _():
            recv[0, field] = jnp.zeros(recv.shape[2:], recv.dtype)

        @pl.when(band < bands - 1)
        def _():
            up.start()

        @pl.when(band == bands - 1)
        def _():
            recv[1, field] = jnp.zeros(recv.shape[2:], recv.dtype)

    def halo_wait(exchange):
        @pl.when(band > 0)
        def _():
            for field in range(fields):
                halo_copies(*exchange, field)[1].wait_recv()

        @pl.when(band < bands - 1)
        def _():
            for field in range(fields):
                halo_copies(*exchange, field)[0].wait_recv()

    def halo_drain(exchange):
        @pl.when(band > 0)
        def _():
            for field in range(fields):
                halo_copies(*exchange, field)[0].wait_send()

        @pl.when(band < bands - 1)
        def _():
            for field in range(fields):
                halo_copies(*exchange, field)[1].wait_send()

    base_halo = (base_send, base_recv, base_ss, base_rs)
    field_halo = (field_send, field_recv, field_ss, field_rs)
    last_halo = (last_send, last_recv, last_ss, last_rs)

    for load in loads[:4]:
        load.wait()

    base_half = stored[chosen[0]]
    base = base_half.astype(jnp.float32)
    base_send[0] = base[:, :halo]
    base_send[1] = base[:, rows - halo :]

    cells = lax.broadcasted_iota(jnp.int32, (columns, station_column.shape[1]), 0)
    at_column = cells == station_column[...]
    local_row = station_row[...] - band * rows
    at_row = (
        lax.broadcasted_iota(jnp.int32, (rows, station_row.shape[1]), 0) == local_row
    )
    one_hot = at_column.astype(jnp.float32).astype(jnp.bfloat16)
    by_row = jnp.dot(
        base_half[0],
        one_hot,
        preferred_element_type=jnp.float32,
    )
    seen = jnp.sum(jnp.where(at_row, by_row, 0.0), axis=0, keepdims=True)
    innovation = seen - station_value[...]
    weight = 1.0 + 2.0 * station_row[...].astype(jnp.float32) / total_rows
    weighted = weight * innovation
    cost = jnp.sum(weighted * innovation, axis=1, keepdims=True) / (2.0 * groups * observed)
    cost_row = jnp.broadcast_to(cost, (1, LANES))
    cost_out[...] = cost_row
    source = jnp.where(at_row, weighted / (2.0 * math.sqrt(observed)), 0.0)
    parts = [source.astype(jnp.bfloat16).astype(jnp.float32)]
    parts.append((source - parts[0]).astype(jnp.bfloat16).astype(jnp.float32))
    parts.append(source - parts[0] - parts[1])
    parts.append(jnp.zeros_like(source))
    placed = lax.dot_general(
        jnp.concatenate(parts, axis=0).astype(jnp.bfloat16),
        one_hot,
        (((1,), (1,)), ((), ())),
        preferred_element_type=jnp.float32,
    )
    forced[0] = placed[:rows] + placed[rows : 2 * rows] + placed[2 * rows : 3 * rows]
    for field in range(1, fields):
        forced[field] = jnp.zeros((rows, columns), jnp.float32)

    eye = lax.broadcasted_iota(jnp.int32, (rank, LANES), 0) == lax.broadcasted_iota(
        jnp.int32, (rank, LANES), 1
    )

    def spread_row(row):
        column = jnp.sum(jnp.where(eye, row, 0.0), axis=1, keepdims=True)
        spread[...] = jnp.broadcast_to(column, (rank, LANES))

    block = 8

    def combined(basis, field):
        def some(index, total):
            for inner in range(2 * block):
                k = index * 2 * block + inner
                factor = jnp.broadcast_to(spread[pl.ds(k, 1), :], (rows, LANES))
                total = total + basis[k, field].astype(jnp.float32) * jnp.concatenate(
                    [factor] * tiles, axis=1
                )
            return total

        return lax.fori_loop(
            0, rank // (2 * block), some, jnp.zeros((rows, columns), jnp.float32)
        )

    def fold(pairs, kept):
        def some(index, carry):
            totals = [None] * block
            for basis, values in pairs:
                for field in range(kept):
                    value = values[field]
                    for inner in range(block):
                        product = basis[index * block + inner, field].astype(jnp.float32) * value
                        for tile in range(tiles):
                            term = product[:, tile * LANES : (tile + 1) * LANES]
                            before = totals[inner]
                            totals[inner] = term if before is None else before + term
            for inner in range(block):
                folded[pl.ds(index * block + inner, 1), :] = jnp.sum(
                    totals[inner], axis=0, keepdims=True
                )
            return carry

        lax.fori_loop(0, rank // block, some, 0)
        share = jnp.sum(folded[...], axis=1, keepdims=True)
        message[...] = jnp.sum(jnp.where(eye, share, 0.0), axis=0, keepdims=True)

    def widen(source, target):
        def some(index, carry):
            for inner in range(2):
                k = index * 2 + inner
                for field in range(fields):
                    target[k, field] = source[k, field].astype(jnp.float32)
            return carry

        lax.fori_loop(0, rank // 2, some, 0)

    loads[4].wait()

    @pl.when(group < last_group)
    def _():
        loads[6].start()
        loads[5].wait()

    @pl.when(group == last_group)
    def _():
        fold(((sketch, forced),), 1)

    pl.semaphore_wait(barrier, greetings)

    def later_copy(offset):
        other = lax.rem(band + offset, bands)
        return remote(
            message,
            later_in.at[band],
            later_ss.at[offset],
            later_rs.at[band],
            {"tm": jnp.maximum(group - 1, 0), "lat": other},
        )

    def own_copy(offset):
        other = lax.rem(band + offset, bands)
        return remote(
            message, own_in.at[band], own_ss.at[offset], own_rs.at[band], {"lat": other}
        )

    def own_arrival(offset):
        other = lax.rem(band + offset, bands)
        return remote(
            message, own_in.at[other], own_ss.at[offset], own_rs.at[other], {"lat": other}
        )

    def announce():
        @pl.when(group > 0)
        def _():
            each(bands, 0, lambda offset: later_copy(offset).start())

        each(bands, 1, lambda offset: own_copy(offset).start())
        own_in[band] = message[...]

    @pl.when(group == last_group)
    def _():
        announce()
        loads[5].wait()

    for field in range(fields):
        halo_start(base_halo, field)

    def cost_copy(offset):
        other = lax.rem(band + offset, bands)
        return remote(
            cost_out, cost_in.at[band], cost_ss.at[offset], cost_rs.at[band], {"lat": other}
        )

    def cost_arrival(offset):
        other = lax.rem(band + offset, bands)
        return remote(
            cost_out, cost_in.at[other], cost_ss.at[offset], cost_rs.at[other], {"lat": other}
        )

    each(bands, 1, lambda offset: cost_copy(offset).start())
    cost_in[band] = cost_row

    def cost_group_copy(offset):
        other = lax.rem(group + offset, groups)
        return remote(
            cost_group_out,
            cost_group_in.at[group],
            cost_group_ss.at[offset],
            cost_group_rs.at[group],
            {"tm": other},
        )

    def cost_group_arrival(offset):
        other = lax.rem(group + offset, groups)
        return remote(
            cost_group_out,
            cost_group_in.at[other],
            cost_group_ss.at[offset],
            cost_group_rs.at[other],
            {"tm": other},
        )

    def share_cost():
        each(bands, 1, lambda offset: cost_arrival(offset).wait_recv())
        group_cost = jnp.sum(cost_in[...], axis=0)
        cost_group_out[...] = group_cost
        each(groups, 1, lambda offset: cost_group_copy(offset).start())
        cost_group_in[group] = group_cost

    low, high = pl.ds(0, halo), pl.ds(halo, halo)
    top = pl.ds(rows - halo, halo)
    beyond_down = remote(
        sketch.at[:, :, low], beyond.at[:, :, low], beyond_ss.at[0], beyond_rs.at[1], below
    )
    beyond_up = remote(
        sketch.at[:, :, top], beyond.at[:, :, high], beyond_ss.at[1], beyond_rs.at[0], above
    )

    def clear(place):
        def one(k, carry):
            for field in range(fields):
                beyond[k, field, place] = jnp.zeros((halo, columns), beyond.dtype)
            return carry

        lax.fori_loop(0, rank, one, 0)

    @pl.when(group == 0)
    def _():
        @pl.when(band > 0)
        def _():
            beyond_down.start()

        @pl.when(band == 0)
        def _():
            clear(high)

        @pl.when(band < bands - 1)
        def _():
            beyond_up.start()

        @pl.when(band == bands - 1)
        def _():
            clear(low)

    @pl.when(group < last_group)
    def _():
        widen(sketch, sketch_wide)
        loads[6].wait()
        widen(test, test_wide)

    halo_wait(base_halo)
    scales = (0.5 * wave_coef * 0.25, 0.5 * flow_coef * 0.4, 0.5 * flow_coef * 0.4)
    starts = (0.5 * wave_coef, 0.0, 0.0)
    for field in range(fields):
        for place, part in (
            (pl.ds(0, rows), base[field]),
            (pl.ds(rows, halo), base_recv[1, field]),
            (pl.ds(rows + halo, halo), base_recv[0, field]),
        ):
            coef_ext[field, place] = starts[field] + scales[field] * part
    span = rows + 2 * halo
    inside = pl.ds(0, rows)
    after, before = pl.ds(rows, halo), pl.ds(rows + halo, halo)
    outside = pl.ds(rows, 2 * halo)

    def march(step_of, keep_outside):
        turned = lax.broadcasted_iota(jnp.int32, (span, LANES), 0)
        where = band * rows + jnp.where(turned < rows + halo, turned, turned - span)
        latitude = where.astype(jnp.float32)
        turn = wave_coef * coriolis_coef * (2.0 * (latitude + 0.5) / total_rows - 1.0)
        keep = jnp.where((where >= 0) & (where < total_rows), 1.0, 0.0)
        lane = lax.broadcasted_iota(jnp.int32, (span, LANES), 1)
        first, last = lane == 0, lane == LANES - 1

        def tiled(ref, field):
            return [ref[field, :, tile * LANES : (tile + 1) * LANES] for tile in range(tiles)]

        def dlon(values):
            ahead = [pltpu.roll(value, LANES - 1, 1) for value in values]
            behind = [pltpu.roll(value, 1, 1) for value in values]
            return [
                jnp.where(last, ahead[(tile + 1) % tiles], ahead[tile])
                - jnp.where(first, behind[tile - 1], behind[tile])
                for tile in range(tiles)
            ]

        coefs = [tiled(coef_ext, field) for field in range(fields)]
        source, target = ext, spare
        for step in range(STEPS):
            short = step == STEPS - 1 and not keep_outside
            state = [tiled(source, field) for field in range(fields)]
            for field, values in step_of(state, coefs, turn, dlon):
                for tile in range(tiles):
                    place = slice(tile * LANES, (tile + 1) * LANES)
                    value = values[tile] * keep
                    if short:
                        target[field, inside, place] = value[:rows]
                    else:
                        target[field, :, place] = value
            source, target = target, source

    def banded(basis, exchange):
        send, recv = exchange[:2]
        for field in range(fields):
            total = combined(basis, field)
            send[0, field] = total[:halo]
            send[1, field] = total[rows - halo :]
            halo_start(exchange, field)
            ext[field, inside] = total
        halo_wait(exchange)
        for field in range(fields):
            ext[field, before] = recv[0, field]
            ext[field, after] = recv[1, field]

    map_factor = map_scale / math.sqrt(rank * fields * total_rows * columns)

    def add_mapped():
        for field in range(fields):
            forced[field] = forced[field] + map_factor * ext[field, inside]

    @pl.when(group < last_group)
    def _():
        def arrive(offset):
            remote(
                message,
                later_in.at[offset],
                later_ss.at[offset],
                later_rs.at[offset],
                {"tm": group, "lat": offset},
            ).wait_recv()

        @pl.when(group == 0)
        def _():
            @pl.when(band > 0)
            def _():
                beyond_up.wait_recv()

            @pl.when(band < bands - 1)
            def _():
                beyond_down.wait_recv()

            widen(beyond, beyond_wide)

        @pl.when(group < last_group - 1)
        def _():
            share_cost()

        each(bands, 0, arrive)
        spread_row(jnp.sum(later_in[...], axis=0))

        @pl.when(group > 0)
        def _():
            banded(test_wide, field_halo)
            march(advance_adjoint, False)
            add_mapped()
            fold(((sketch_wide, forced),), fields)

        @pl.when(group == 0)
        def _():
            for field in range(fields):
                ext[field, inside] = combined(test_wide, field)
                ext[field, outside] = jnp.zeros((2 * halo, columns), jnp.float32)
            march(advance_adjoint, True)
            add_mapped()
            for field in range(fields):
                forced_beyond[field] = map_factor * ext[field, outside]

            fold(((sketch_wide, forced), (beyond_wide, forced_beyond)), fields)

        announce()

    @pl.when(group >= last_group - 1)
    def _():
        share_cost()

    each(groups, 1, lambda offset: cost_group_arrival(offset).wait_recv())
    cost_here[...] = jnp.sum(cost_group_in[...], axis=0)[:, :1]
    cost_store = pltpu.make_async_copy(cost_here, total_cost, load_sem.at[7])
    cost_store.start()

    each(bands, 1, lambda offset: own_arrival(offset).wait_recv())
    adjoint_row = jnp.sum(own_in[...], axis=0)
    adjoint[...] = adjoint_row[:, :rank]
    spread_row(adjoint_row)

    @pl.when(group > 0)
    def _():
        banded(sketch, last_halo)

    @pl.when(group == 0)
    def _():
        for field in range(fields):
            ext[field, inside] = combined(sketch_wide, field)
            ext[field, outside] = combined(beyond_wide, field)

    march(advance, False)
    for field in range(fields):
        increment[0, field] = ext[field, inside] / math.sqrt(rank)

    cost_store.wait()

    halo_drain(base_halo)
    each(bands, 1, lambda offset: cost_copy(offset).wait_send())
    each(bands, 1, lambda offset: own_copy(offset).wait_send())
    each(groups, 1, lambda offset: cost_group_copy(offset).wait_send())

    @pl.when(group > 0)
    def _():
        halo_drain(last_halo)
        each(bands, 0, lambda offset: later_copy(offset).wait_send())

    @pl.when((group > 0) & (group < last_group))
    def _():
        halo_drain(field_halo)

    @pl.when(group == 0)
    def _():
        @pl.when(band > 0)
        def _():
            beyond_down.wait_send()

        @pl.when(band < bands - 1)
        def _():
            beyond_up.wait_send()


def body(
    groups,
    bands,
    sketch,
    test_sketch,
    checkpoints,
    checkpoint_step,
    station_row,
    station_column,
    station_value,
):
    rank, fields, rows, columns = sketch.shape
    span = rows + 2 * STEPS
    f32 = jnp.float32

    def in_hbm(array):
        return pltpu.with_memory_space_constraint(array, pltpu.HBM)

    vmem = pl.BlockSpec(memory_space=pltpu.VMEM)
    hbm = pl.BlockSpec(memory_space=pltpu.HBM)
    edge = pltpu.VMEM((2, fields, STEPS, columns), f32)
    dma = pltpu.SemaphoreType.DMA
    increment, adjoint, cost = pl.pallas_call(
        functools.partial(kernel, groups, bands),
        out_shape=(
            jax.ShapeDtypeStruct((1, fields, rows, columns), f32),
            jax.ShapeDtypeStruct((1, rank), f32),
            jax.ShapeDtypeStruct((1, 1), f32),
        ),
        in_specs=[hbm, hbm, hbm, pl.BlockSpec(memory_space=pltpu.SMEM), hbm, hbm, hbm],
        out_specs=(vmem, vmem, hbm),
        scratch_shapes=[
            pltpu.VMEM(sketch.shape, sketch.dtype),
            pltpu.VMEM(test_sketch.shape, test_sketch.dtype),
            pltpu.VMEM((rank, fields, 2 * STEPS, columns), sketch.dtype),
            pltpu.VMEM(sketch.shape, f32),
            pltpu.VMEM(test_sketch.shape, f32),
            pltpu.VMEM((rank, fields, 2 * STEPS, columns), f32),
            pltpu.VMEM(checkpoints.shape, checkpoints.dtype),
            pltpu.VMEM(station_row.shape, station_row.dtype),
            pltpu.VMEM(station_column.shape, station_column.dtype),
            pltpu.VMEM(station_value.shape, station_value.dtype),
            pltpu.VMEM((fields, span, columns), f32),
            pltpu.VMEM((fields, span, columns), f32),
            pltpu.VMEM((fields, span, columns), f32),
            pltpu.VMEM((fields, rows, columns), f32),
            pltpu.VMEM((fields, 2 * STEPS, columns), f32),
            pltpu.VMEM((rank, LANES), f32),
            pltpu.VMEM((rank, LANES), f32),
            edge,
            edge,
            edge,
            edge,
            edge,
            edge,
            pltpu.VMEM((1, LANES), f32),
            pltpu.VMEM((bands, 1, LANES), f32),
            pltpu.VMEM((bands, 1, LANES), f32),
            pltpu.VMEM((1, LANES), f32),
            pltpu.VMEM((bands, 1, LANES), f32),
            pltpu.VMEM((1, LANES), f32),
            pltpu.VMEM((groups, 1, LANES), f32),
            pltpu.VMEM((1, 1), f32),
            dma((8,)),
            dma((2,)),
            dma((2,)),
            dma((2, fields)),
            dma((2, fields)),
            dma((2, fields)),
            dma((2, fields)),
            dma((2, fields)),
            dma((2, fields)),
            dma((bands,)),
            dma((bands,)),
            dma((bands,)),
            dma((bands,)),
            dma((bands,)),
            dma((bands,)),
            dma((groups,)),
            dma((groups,)),
        ],
        compiler_params=pltpu.CompilerParams(
            collective_id=0,
            has_side_effects=True,
            vmem_limit_bytes=48 * 1024 * 1024,
        ),
    )(
        in_hbm(sketch),
        in_hbm(test_sketch),
        in_hbm(checkpoints),
        checkpoint_step,
        in_hbm(station_row),
        in_hbm(station_column),
        in_hbm(station_value),
    )
    return increment, adjoint, cost[0, 0]


def solution(mesh):
    placed = (
        P("tm", None, "lat", None),
        P("tm", None, "lat", None),
        P("tm", None, "lat", None),
        P("tm"),
        P("tm", "lat"),
        P("tm", "lat"),
        P("tm", "lat"),
    )
    return jax.shard_map(
        functools.partial(body, mesh.shape["tm"], mesh.shape["lat"]),
        mesh=mesh,
        in_specs=placed,
        out_specs=(P("tm", None, "lat", None), P("tm", None), P()),
        check_vma=False,
    )
```

profile of v0, /device:TPU:0, one launch (start us, length us, event | category | flops | bytes accessed | tf_op | source)
XLA Modules:
  0.0 37.9 jit_solution(5872461986216689283)
XLA Ops:
  1.3 33.7 %shard_map.94 = (f32[1,3,8,1024]{3,2,1,0:T(8,128)S(1)}, f32[1,64]{1,0:T(1,128)S(1)}, f32[1,1]{1,0:T(1,128)}) custom-call(bf16[64,3,8,1024]{3,2,1,0:T(8,128)(2,1)} %sketch_hbm.1, bf16[64,3,8,1024]{3,2,1,0:T(8,128)(2,1)} %test_hbm.1, bf16[4,3,8,1024]{3,2,1,0:T(8,128)(2,1)} %stored_hbm.1, s32[1]{0:T(128)S(6)} %copy.13.chosen, s32[1,128]{1,0:T(1,128)} %row_hbm.1, ...), custom_call_target="tpu_custom_call" | custom-call | tf_op jit(solution)/shard_map/pallas_call | solution.py:682
  35.0 0.6 %copy.14 = f32[1,3,8,1024]{3,2,1,0:T(8,128)} copy(f32[1,3,8,1024]{3,2,1,0:T(8,128)S(1)} %get-tuple-element.12) | data formatting | bytes 196608
  35.7 0.5 %copy.15 = f32[1,64]{1,0:T(1,128)} copy(f32[1,64]{1,0:T(1,128)S(1)} %get-tuple-element.13) | data formatting | bytes 512
where the time goes:
time: 38 us; the launch traced here: 37.9 us
  Pallas kernels  33.7 us (89%)
  between operations  2.97 us (8%)
  local copies, waits for them, and re-layouts  1.15 us (3%)
    pallas_call x1, Pallas kernels, body(): pl.pallas_call(functools.partial(kernel, groups, bands), out_shape=(jax.S...  33.7 us
    unnamed x2, local copies, waits for them, and re-layouts  1.15 us

commit v1 on v0

--- a/solution.py
+++ b/solution.py
@@ -197,10 +197,8 @@
     above = {"lat": jnp.minimum(band + 1, bands - 1)}
 
     def halo_copies(send, recv, ss, rs, field):
-        down = remote(
-            send.at[0, field], recv.at[1, field], ss.at[0, field], rs.at[1, field], below
-        )
-        up = remote(send.at[1, field], recv.at[0, field], ss.at[1, field], rs.at[0, field], above)
+        down = remote(send.at[0, field], recv.at[1, field], ss.at[0], rs.at[0], below)
+        up = remote(send.at[1, field], recv.at[0, field], ss.at[0], rs.at[0], above)
         return down, up
 
     def halo_start(exchange, field):
@@ -223,27 +221,34 @@
         def _():
             recv[1, field] = jnp.zeros(recv.shape[2:], recv.dtype)
 
+    def both_or_one(action):
+        @pl.when((band > 0) & (band < bands - 1))
+        def _():
+            action(slice(None))
+
+        @pl.when(band == 0)
+        def _():
+            action(1)
+
+        @pl.when(band == bands - 1)
+        def _():
+            action(0)
+
     def halo_wait(exchange):
-        @pl.when(band > 0)
-        def _():
-            for field in range(fields):
-                halo_copies(*exchange, field)[1].wait_recv()
-
-        @pl.when(band < bands - 1)
-        def _():
-            for field in range(fields):
-                halo_copies(*exchange, field)[0].wait_recv()
+        _, recv, ss, rs = exchange
+
+        def one(place):
+            remote(recv.at[place], recv.at[place], ss.at[0], rs.at[0], above).wait_recv()
+
+        both_or_one(one)
 
     def halo_drain(exchange):
-        @pl.when(band > 0)
-        def _():
-            for field in range(fields):
-                halo_copies(*exchange, field)[0].wait_send()
-
-        @pl.when(band < bands - 1)
-        def _():
-            for field in range(fields):
-                halo_copies(*exchange, field)[1].wait_send()
+        send, _, ss, rs = exchange
+
+        def one(place):
+            remote(send.at[place], send.at[place], ss.at[0], rs.at[0], above).wait_send()
+
+        both_or_one(one)
 
     base_halo = (base_send, base_recv, base_ss, base_rs)
     field_halo = (field_send, field_recv, field_ss, field_rs)
@@ -337,7 +342,7 @@
         share = jnp.sum(folded[...], axis=1, keepdims=True)
         message[...] = jnp.sum(jnp.where(eye, share, 0.0), axis=0, keepdims=True)
 
-    def widen(source, target):
+    def widen(source, target, start, stop):
         def some(index, carry):
             for inner in range(2):
                 k = index * 2 + inner
@@ -345,7 +350,7 @@
                     target[k, field] = source[k, field].astype(jnp.float32)
             return carry
 
-        lax.fori_loop(0, rank // 2, some, 0)
+        lax.fori_loop(start // 2, stop // 2, some, 0)
 
     loads[4].wait()
 
@@ -365,22 +370,20 @@
         return remote(
             message,
             later_in.at[band],
-            later_ss.at[offset],
-            later_rs.at[band],
+            later_ss.at[0],
+            later_rs.at[0],
             {"tm": jnp.maximum(group - 1, 0), "lat": other},
         )
 
     def own_copy(offset):
         other = lax.rem(band + offset, bands)
         return remote(
-            message, own_in.at[band], own_ss.at[offset], own_rs.at[band], {"lat": other}
-        )
-
-    def own_arrival(offset):
-        other = lax.rem(band + offset, bands)
-        return remote(
-            message, own_in.at[other], own_ss.at[offset], own_rs.at[other], {"lat": other}
-        )
+            message, own_in.at[band], own_ss.at[0], own_rs.at[0], {"lat": other}
+        )
+
+    def group_end(buffer, count, ss, rs):
+        place = buffer.at[pl.ds(0, count)]
+        return remote(place, place, ss.at[0], rs.at[0], {"lat": lax.rem(band + 1, bands)})
 
     def announce():
         @pl.when(group > 0)
@@ -401,13 +404,7 @@
     def cost_copy(offset):
         other = lax.rem(band + offset, bands)
         return remote(
-            cost_out, cost_in.at[band], cost_ss.at[offset], cost_rs.at[band], {"lat": other}
-        )
-
-    def cost_arrival(offset):
-        other = lax.rem(band + offset, bands)
-        return remote(
-            cost_out, cost_in.at[other], cost_ss.at[offset], cost_rs.at[other], {"lat": other}
+            cost_out, cost_in.at[band], cost_ss.at[0], cost_rs.at[0], {"lat": other}
         )
 
     each(bands, 1, lambda offset: cost_copy(offset).start())
@@ -418,23 +415,13 @@
         return remote(
             cost_group_out,
             cost_group_in.at[group],
-            cost_group_ss.at[offset],
-            cost_group_rs.at[group],
+            cost_group_ss.at[0],
+            cost_group_rs.at[0],
             {"tm": other},
         )
 
-    def cost_group_arrival(offset):
-        other = lax.rem(group + offset, groups)
-        return remote(
-            cost_group_out,
-            cost_group_in.at[other],
-            cost_group_ss.at[offset],
-            cost_group_rs.at[other],
-            {"tm": other},
-        )
-
     def share_cost():
-        each(bands, 1, lambda offset: cost_arrival(offset).wait_recv())
+        group_end(cost_in, bands - 1, cost_ss, cost_rs).wait_recv()
         group_cost = jnp.sum(cost_in[...], axis=0)
         cost_group_out[...] = group_cost
         each(groups, 1, lambda offset: cost_group_copy(offset).start())
@@ -442,12 +429,46 @@
 
     low, high = pl.ds(0, halo), pl.ds(halo, halo)
     top = pl.ds(rows - halo, halo)
-    beyond_down = remote(
-        sketch.at[:, :, low], beyond.at[:, :, low], beyond_ss.at[0], beyond_rs.at[1], below
-    )
-    beyond_up = remote(
-        sketch.at[:, :, top], beyond.at[:, :, high], beyond_ss.at[1], beyond_rs.at[0], above
-    )
+    early = rank * 3 // 4
+    lots = (pl.ds(0, early), pl.ds(early, rank - early))
+
+    def beyond_copies(lot):
+        columns_of = lots[lot]
+        return (
+            remote(
+                sketch.at[columns_of, :, low],
+                beyond.at[columns_of, :, low],
+                beyond_ss.at[lot],
+                beyond_rs.at[lot],
+                below,
+            ),
+            remote(
+                sketch.at[columns_of, :, top],
+                beyond.at[columns_of, :, high],
+                beyond_ss.at[lot],
+                beyond_rs.at[lot],
+                above,
+            ),
+        )
+
+    def beyond_end(lot):
+        ends = {}
+
+        def one(place):
+            rows_of = pl.ds(0, 2 * halo) if isinstance(place, slice) else low
+            part = beyond.at[lots[lot], :, rows_of]
+            ends[0] = remote(part, part, beyond_ss.at[lot], beyond_rs.at[lot], above)
+
+        return one, ends
+
+    def beyond_wait(lot, sent):
+        one, ends = beyond_end(lot)
+
+        def wait(place):
+            one(place)
+            ends[0].wait_send() if sent else ends[0].wait_recv()
+
+        both_or_one(wait)
 
     def clear(place):
         def one(k, carry):
@@ -461,7 +482,8 @@
     def _():
         @pl.when(band > 0)
         def _():
-            beyond_down.start()
+            for lot in range(2):
+                beyond_copies(lot)[0].start()
 
         @pl.when(band == 0)
         def _():
@@ -469,7 +491,8 @@
 
         @pl.when(band < bands - 1)
         def _():
-            beyond_up.start()
+            for lot in range(2):
+                beyond_copies(lot)[1].start()
 
         @pl.when(band == bands - 1)
         def _():
@@ -477,9 +500,9 @@
 
     @pl.when(group < last_group)
     def _():
-        widen(sketch, sketch_wide)
+        widen(sketch, sketch_wide, 0, rank)
         loads[6].wait()
-        widen(test, test_wide)
+        widen(test, test_wide, 0, rank)
 
     halo_wait(base_halo)
     scales = (0.5 * wave_coef * 0.25, 0.5 * flow_coef * 0.4, 0.5 * flow_coef * 0.4)
@@ -553,32 +576,18 @@
 
     @pl.when(group < last_group)
     def _():
-        def arrive(offset):
-            remote(
-                message,
-                later_in.at[offset],
-                later_ss.at[offset],
-                later_rs.at[offset],
-                {"tm": group, "lat": offset},
-            ).wait_recv()
+        @pl.when(group < last_group - 1)
+        def _():
+            share_cost()
 
         @pl.when(group == 0)
         def _():
-            @pl.when(band > 0)
-            def _():
-                beyond_up.wait_recv()
-
-            @pl.when(band < bands - 1)
-            def _():
-                beyond_down.wait_recv()
-
-            widen(beyond, beyond_wide)
-
-        @pl.when(group < last_group - 1)
-        def _():
-            share_cost()
-
-        each(bands, 0, arrive)
+            beyond_wait(0, False)
+            widen(beyond, beyond_wide, 0, early)
+            beyond_wait(1, False)
+            widen(beyond, beyond_wide, early, rank)
+
+        group_end(later_in, bands, later_ss, later_rs).wait_recv()
         spread_row(jnp.sum(later_in[...], axis=0))
 
         @pl.when(group > 0)
@@ -606,12 +615,12 @@
     def _():
         share_cost()
 
-    each(groups, 1, lambda offset: cost_group_arrival(offset).wait_recv())
+    group_end(cost_group_in, groups - 1, cost_group_ss, cost_group_rs).wait_recv()
     cost_here[...] = jnp.sum(cost_group_in[...], axis=0)[:, :1]
     cost_store = pltpu.make_async_copy(cost_here, total_cost, load_sem.at[7])
     cost_store.start()
 
-    each(bands, 1, lambda offset: own_arrival(offset).wait_recv())
+    group_end(own_in, bands - 1, own_ss, own_rs).wait_recv()
     adjoint_row = jnp.sum(own_in[...], axis=0)
     adjoint[...] = adjoint_row[:, :rank]
     spread_row(adjoint_row)
@@ -633,14 +642,14 @@
     cost_store.wait()
 
     halo_drain(base_halo)
-    each(bands, 1, lambda offset: cost_copy(offset).wait_send())
-    each(bands, 1, lambda offset: own_copy(offset).wait_send())
-    each(groups, 1, lambda offset: cost_group_copy(offset).wait_send())
+    group_end(cost_in, bands - 1, cost_ss, cost_rs).wait_send()
+    group_end(own_in, bands - 1, own_ss, own_rs).wait_send()
+    group_end(cost_group_in, groups - 1, cost_group_ss, cost_group_rs).wait_send()
 
     @pl.when(group > 0)
     def _():
         halo_drain(last_halo)
-        each(bands, 0, lambda offset: later_copy(offset).wait_send())
+        group_end(later_in, bands, later_ss, later_rs).wait_send()
 
     @pl.when((group > 0) & (group < last_group))
     def _():
@@ -648,13 +657,8 @@
 
     @pl.when(group == 0)
     def _():
-        @pl.when(band > 0)
-        def _():
-            beyond_down.wait_send()
-
-        @pl.when(band < bands - 1)
-        def _():
-            beyond_up.wait_send()
+        for lot in range(2):
+            beyond_wait(lot, True)
 
 
 def body(
@@ -723,20 +727,20 @@
             dma((8,)),
             dma((2,)),
             dma((2,)),
-            dma((2, fields)),
-            dma((2, fields)),
-            dma((2, fields)),
-            dma((2, fields)),
-            dma((2, fields)),
-            dma((2, fields)),
-            dma((bands,)),
-            dma((bands,)),
-            dma((bands,)),
-            dma((bands,)),
-            dma((bands,)),
-            dma((bands,)),
-            dma((groups,)),
-            dma((groups,)),
+            dma((1,)),
+            dma((1,)),
+            dma((1,)),
+            dma((1,)),
+            dma((1,)),
+            dma((1,)),
+            dma((1,)),
+            dma((1,)),
+            dma((1,)),
+            dma((1,)),
+            dma((1,)),
+            dma((1,)),
+            dma((1,)),
+            dma((1,)),
         ],
         compiler_params=pltpu.CompilerParams(
             collective_id=0,

time: 38 us -> 37.3 us (0.982)
  Pallas kernels: 33.7 us -> 33 us
    pallas_call x1, Pallas kernels: 33.7 us -> 33 us  [body(): pl.pallas_call(functools.partial(kernel, groups, bands), out_shape=(jax.S...]
where the time goes in v1:
time: 37.3 us; the launch traced here: 37.1 us
  Pallas kernels  33 us (88%)
  between operations  2.97 us (8%)
  local copies, waits for them, and re-layouts  1.15 us (3%)
    pallas_call x1, Pallas kernels, body(): pl.pallas_call(functools.partial(kernel, groups, bands), out_shape=(jax.S...  33 us
    unnamed x2, local copies, waits for them, and re-layouts  1.15 us

profile of v1, /device:TPU:0, one launch (start us, length us, event | category | flops | bytes accessed | tf_op | source)
XLA Modules:
  0.0 37.1 jit_solution(16916118274110458388)
XLA Ops:
  1.3 33.0 %shard_map.94 = (f32[1,3,8,1024]{3,2,1,0:T(8,128)S(1)}, f32[1,64]{1,0:T(1,128)S(1)}, f32[1,1]{1,0:T(1,128)}) custom-call(bf16[64,3,8,1024]{3,2,1,0:T(8,128)(2,1)} %sketch_hbm.1, bf16[64,3,8,1024]{3,2,1,0:T(8,128)(2,1)} %test_hbm.1, bf16[4,3,8,1024]{3,2,1,0:T(8,128)(2,1)} %stored_hbm.1, s32[1]{0:T(128)S(6)} %copy.13.chosen, s32[1,128]{1,0:T(1,128)} %row_hbm.1, ...), custom_call_target="tpu_custom_call" | custom-call | tf_op jit(solution)/shard_map/pallas_call | solution.py:686
  34.3 0.6 %copy.14 = f32[1,3,8,1024]{3,2,1,0:T(8,128)} copy(f32[1,3,8,1024]{3,2,1,0:T(8,128)S(1)} %get-tuple-element.12) | data formatting | bytes 196608
  34.9 0.5 %copy.15 = f32[1,64]{1,0:T(1,128)} copy(f32[1,64]{1,0:T(1,128)S(1)} %get-tuple-element.13) | data formatting | bytes 512

commit v2 on v1

--- a/solution.py
+++ b/solution.py
@@ -77,7 +77,6 @@
     value_hbm,
     increment,
     adjoint,
-    total_cost,
     sketch,
     test,
     beyond,
@@ -617,12 +616,10 @@
 
     group_end(cost_group_in, groups - 1, cost_group_ss, cost_group_rs).wait_recv()
     cost_here[...] = jnp.sum(cost_group_in[...], axis=0)[:, :1]
-    cost_store = pltpu.make_async_copy(cost_here, total_cost, load_sem.at[7])
-    cost_store.start()
-
     group_end(own_in, bands - 1, own_ss, own_rs).wait_recv()
     adjoint_row = jnp.sum(own_in[...], axis=0)
-    adjoint[...] = adjoint_row[:, :rank]
+    here = lax.broadcasted_iota(jnp.int32, (1, LANES), 1)
+    adjoint[...] = jnp.where(here == rank, cost_here[...], adjoint_row)
     spread_row(adjoint_row)
 
     @pl.when(group > 0)
@@ -638,8 +635,6 @@
     march(advance, False)
     for field in range(fields):
         increment[0, field] = ext[field, inside] / math.sqrt(rank)
-
-    cost_store.wait()
 
     halo_drain(base_halo)
     group_end(cost_in, bands - 1, cost_ss, cost_rs).wait_send()
@@ -683,15 +678,14 @@
     hbm = pl.BlockSpec(memory_space=pltpu.HBM)
     edge = pltpu.VMEM((2, fields, STEPS, columns), f32)
     dma = pltpu.SemaphoreType.DMA
-    increment, adjoint, cost = pl.pallas_call(
+    increment, packed = pl.pallas_call(
         functools.partial(kernel, groups, bands),
         out_shape=(
             jax.ShapeDtypeStruct((1, fields, rows, columns), f32),
-            jax.ShapeDtypeStruct((1, rank), f32),
-            jax.ShapeDtypeStruct((1, 1), f32),
+            jax.ShapeDtypeStruct((1, LANES), f32),
         ),
         in_specs=[hbm, hbm, hbm, pl.BlockSpec(memory_space=pltpu.SMEM), hbm, hbm, hbm],
-        out_specs=(vmem, vmem, hbm),
+        out_specs=(vmem, vmem),
         scratch_shapes=[
             pltpu.VMEM(sketch.shape, sketch.dtype),
             pltpu.VMEM(test_sketch.shape, test_sketch.dtype),
@@ -756,7 +750,8 @@
         in_hbm(station_column),
         in_hbm(station_value),
     )
-    return increment, adjoint, cost[0, 0]
+    keep = lax.broadcasted_iota(jnp.int32, packed.shape, 1) == rank
+    return increment, packed[:, :rank], jnp.sum(jnp.where(keep, packed, 0.0))
 
 
 def solution(mesh):

time: 37.3 us -> 36.2 us (0.971)
  between operations: 2.97 us -> 1.29 us
  other arithmetic: 0 us -> 0.6 us
    reduce_sum x0 -> x1, other arithmetic: none -> 0.6 us  [body(): return (increment, packed[:, :rank], jnp.sum(jnp.where(keep, packed, 0.0)))]
where the time goes in v2:
time: 36.2 us; the launch traced here: 36 us
  Pallas kernels  33 us (91%)
  between operations  1.29 us (4%)
  local copies, waits for them, and re-layouts  1.15 us (3%)
  other arithmetic  0.6 us (2%)
    pallas_call x1, Pallas kernels, body(): pl.pallas_call(functools.partial(kernel, groups, bands), out_shape=(jax.S...  33 us
    unnamed x2, local copies, waits for them, and re-layouts  1.15 us

profile of v2, /device:TPU:0, one launch (start us, length us, event | category | flops | bytes accessed | tf_op | source)
XLA Modules:
  0.0 36.0 jit_solution(5527895954214540385)
XLA Ops:
  1.3 33.0 %shard_map.94 = (f32[1,3,8,1024]{3,2,1,0:T(8,128)S(1)}, f32[1,128]{1,0:T(1,128)S(1)}) custom-call(bf16[64,3,8,1024]{3,2,1,0:T(8,128)(2,1)} %sketch_hbm.1, bf16[64,3,8,1024]{3,2,1,0:T(8,128)(2,1)} %test_hbm.1, bf16[4,3,8,1024]{3,2,1,0:T(8,128)(2,1)} %stored_hbm.1, s32[1]{0:T(128)S(6)} %copy.12.chosen, s32[1,128]{1,0:T(1,128)} %row_hbm.1, ...), custom_call_target="tpu_custom_call" | custom-call | tf_op jit(solution)/shard_map/pallas_call | solution.py:681
  34.3 0.6 %fusion = f32[]{:T(128)} fusion(f32[1,128]{1,0:T(1,128)S(1)} %get-tuple-element.6), kind=kLoop, calls=%fused_computation.1 | loop fusion | flops 383 | bytes 516 | tf_op jit(solution)/shard_map/reduce_sum | solution.py:754
  34.9 0.6 %copy.13 = f32[1,3,8,1024]{3,2,1,0:T(8,128)} copy(f32[1,3,8,1024]{3,2,1,0:T(8,128)S(1)} %get-tuple-element.10) | data formatting | bytes 196608
  35.5 0.5 %copy.14 = f32[1,64]{1,0:T(1,128)} copy(f32[1,64]{1,0:T(1,128)S(1)} %bitcast.1) | data formatting | bytes 512

commit v3 on v2

--- a/solution.py
+++ b/solution.py
@@ -83,6 +83,7 @@
     sketch_wide,
     test_wide,
     beyond_wide,
+    beyond_rows,
     stored,
     station_row,
     station_column,
@@ -299,9 +300,42 @@
         jnp.int32, (rank, LANES), 1
     )
 
-    def spread_row(row):
+    per_tile = LANES // rows
+    same_column = (
+        lax.broadcasted_iota(jnp.int32, (per_tile, LANES), 1) // rows
+        == lax.broadcasted_iota(jnp.int32, (per_tile, LANES), 0)
+    )
+    same_row = lax.broadcasted_iota(jnp.int32, (rows, LANES), 0) == lax.rem(
+        lax.broadcasted_iota(jnp.int32, (rows, LANES), 1), rows
+    )
+
+    def spread_row(row, doubled):
         column = jnp.sum(jnp.where(eye, row, 0.0), axis=1, keepdims=True)
         spread[...] = jnp.broadcast_to(column, (rank, LANES))
+        if not doubled:
+            return None
+        parts = []
+        for tile in range(rank // per_tile):
+            part = column[tile * per_tile : (tile + 1) * per_tile]
+            line = jnp.sum(jnp.where(same_column, part, 0.0), axis=0, keepdims=True)
+            square = jnp.where(same_row, line, 0.0)
+            coarse = square.astype(jnp.bfloat16).astype(jnp.float32)
+            parts.append(
+                jnp.concatenate([coarse, square - coarse], axis=0).astype(jnp.bfloat16)
+            )
+        return jnp.concatenate(parts, axis=1)
+
+    def by_matmul(left, basis_rows, field):
+        both = jnp.dot(left, basis_rows[field], preferred_element_type=jnp.float32)
+        return both[:rows] + both[rows:]
+
+    def by_vector(basis, field):
+        total = None
+        for k in range(rank):
+            factor = jnp.broadcast_to(spread[pl.ds(k, 1), :], (rows, LANES))
+            term = basis[k, field].astype(jnp.float32) * jnp.concatenate([factor] * tiles, axis=1)
+            total = term if total is None else total + term
+        return total
 
     block = 8
 
@@ -319,7 +353,7 @@
             0, rank // (2 * block), some, jnp.zeros((rows, columns), jnp.float32)
         )
 
-    def fold(pairs, kept):
+    def fold_range(pairs, kept, start, stop):
         def some(index, carry):
             totals = [None] * block
             for basis, values in pairs:
@@ -337,16 +371,29 @@
                 )
             return carry
 
-        lax.fori_loop(0, rank // block, some, 0)
+        lax.fori_loop(start // block, stop // block, some, 0)
+
+    def fold_end():
         share = jnp.sum(folded[...], axis=1, keepdims=True)
         message[...] = jnp.sum(jnp.where(eye, share, 0.0), axis=0, keepdims=True)
 
-    def widen(source, target, start, stop):
+    def widen(source, target, paired, start, stop):
+        kept = 0 if paired is None else paired.shape[0]
+
         def some(index, carry):
+            wides = []
             for inner in range(2):
                 k = index * 2 + inner
-                for field in range(fields):
-                    target[k, field] = source[k, field].astype(jnp.float32)
+                wide = [source[k, field].astype(jnp.float32) for field in range(fields)]
+                if target is not None:
+                    for field in range(fields):
+                        target[k, field] = wide[field]
+                wides.append(wide)
+            place = pl.ds(pl.multiple_of(index * 2 * rows, 2 * rows), 2 * rows)
+            for field in range(kept):
+                paired[field, place] = jnp.concatenate(
+                    [wide[field] for wide in wides], axis=0
+                ).astype(jnp.bfloat16)
             return carry
 
         lax.fori_loop(start // 2, stop // 2, some, 0)
@@ -360,7 +407,8 @@
 
     @pl.when(group == last_group)
     def _():
-        fold(((sketch, forced),), 1)
+        fold_range(((sketch, forced),), 1, 0, rank)
+        fold_end()
 
     pl.semaphore_wait(barrier, greetings)
 
@@ -428,7 +476,7 @@
 
     low, high = pl.ds(0, halo), pl.ds(halo, halo)
     top = pl.ds(rows - halo, halo)
-    early = rank * 3 // 4
+    early = rank * 3 // 4 // block * block
     lots = (pl.ds(0, early), pl.ds(early, rank - early))
 
     def beyond_copies(lot):
@@ -499,9 +547,9 @@
 
     @pl.when(group < last_group)
     def _():
-        widen(sketch, sketch_wide, 0, rank)
+        widen(sketch, sketch_wide, None, 0, rank)
         loads[6].wait()
-        widen(test, test_wide, 0, rank)
+        widen(test, test_wide, None, 0, rank)
 
     halo_wait(base_halo)
     scales = (0.5 * wave_coef * 0.25, 0.5 * flow_coef * 0.4, 0.5 * flow_coef * 0.4)
@@ -554,10 +602,10 @@
                         target[field, :, place] = value
             source, target = target, source
 
-    def banded(basis, exchange):
+    def banded(total_of, exchange):
         send, recv = exchange[:2]
         for field in range(fields):
-            total = combined(basis, field)
+            total = total_of(field)
             send[0, field] = total[:halo]
             send[1, field] = total[rows - halo :]
             halo_start(exchange, field)
@@ -582,19 +630,18 @@
         @pl.when(group == 0)
         def _():
             beyond_wait(0, False)
-            widen(beyond, beyond_wide, 0, early)
-            beyond_wait(1, False)
-            widen(beyond, beyond_wide, early, rank)
+            widen(beyond, beyond_wide, beyond_rows, 0, early)
 
         group_end(later_in, bands, later_ss, later_rs).wait_recv()
-        spread_row(jnp.sum(later_in[...], axis=0))
+        spread_row(jnp.sum(later_in[...], axis=0), False)
 
         @pl.when(group > 0)
         def _():
-            banded(test_wide, field_halo)
+            banded(lambda field: combined(test_wide, field), field_halo)
             march(advance_adjoint, False)
             add_mapped()
-            fold(((sketch_wide, forced),), fields)
+            fold_range(((sketch_wide, forced),), fields, 0, rank)
+            fold_end()
 
         @pl.when(group == 0)
         def _():
@@ -606,9 +653,20 @@
             for field in range(fields):
                 forced_beyond[field] = map_factor * ext[field, outside]
 
-            fold(((sketch_wide, forced), (beyond_wide, forced_beyond)), fields)
+            fold_range(
+                ((sketch_wide, forced), (beyond_wide, forced_beyond)), fields, 0, early
+            )
+            beyond_wait(1, False)
+            fold_range(
+                ((sketch_wide, forced), (beyond, forced_beyond)), fields, early, rank
+            )
+            fold_end()
 
         announce()
+
+    @pl.when(group == 0)
+    def _():
+        widen(beyond, None, beyond_rows, early, rank)
 
     @pl.when(group >= last_group - 1)
     def _():
@@ -618,19 +676,20 @@
     cost_here[...] = jnp.sum(cost_group_in[...], axis=0)[:, :1]
     group_end(own_in, bands - 1, own_ss, own_rs).wait_recv()
     adjoint_row = jnp.sum(own_in[...], axis=0)
+    left_own = spread_row(adjoint_row, True)
     here = lax.broadcasted_iota(jnp.int32, (1, LANES), 1)
     adjoint[...] = jnp.where(here == rank, cost_here[...], adjoint_row)
-    spread_row(adjoint_row)
 
     @pl.when(group > 0)
     def _():
-        banded(sketch, last_halo)
+        banded(lambda field: combined(sketch, field), last_halo)
 
     @pl.when(group == 0)
     def _():
         for field in range(fields):
-            ext[field, inside] = combined(sketch_wide, field)
-            ext[field, outside] = combined(beyond_wide, field)
+            ext[field, outside] = by_matmul(left_own, beyond_rows, field)
+            own = sketch if field == fields - 1 else sketch_wide
+            ext[field, inside] = by_vector(own, field)
 
     march(advance, False)
     for field in range(fields):
@@ -693,6 +752,7 @@
             pltpu.VMEM(sketch.shape, f32),
             pltpu.VMEM(test_sketch.shape, f32),
             pltpu.VMEM((rank, fields, 2 * STEPS, columns), f32),
+            pltpu.VMEM((fields, rank * 2 * STEPS, columns), sketch.dtype),
             pltpu.VMEM(checkpoints.shape, checkpoints.dtype),
             pltpu.VMEM(station_row.shape, station_row.dtype),
             pltpu.VMEM(station_column.shape, station_column.dtype),

time: 36.2 us -> 36 us (level)
  no operation moved by 1% of the time
where the time goes in v3:
time: 36 us; the launch traced here: 35.9 us
  Pallas kernels  32.8 us (91%)
  between operations  1.29 us (4%)
  local copies, waits for them, and re-layouts  1.15 us (3%)
  other arithmetic  0.6 us (2%)
    pallas_call x1, Pallas kernels, body(): pl.pallas_call(functools.partial(kernel, groups, bands), out_shape=(jax.S...  32.8 us
    unnamed x2, local copies, waits for them, and re-layouts  1.15 us

profile of v3, /device:TPU:0, one launch (start us, length us, event | category | flops | bytes accessed | tf_op | source)
XLA Modules:
  0.0 35.9 jit_solution(12145235737977715284)
XLA Ops:
  1.3 32.8 %shard_map.94 = (f32[1,3,8,1024]{3,2,1,0:T(8,128)S(1)}, f32[1,128]{1,0:T(1,128)S(1)}) custom-call(bf16[64,3,8,1024]{3,2,1,0:T(8,128)(2,1)} %sketch_hbm.1, bf16[64,3,8,1024]{3,2,1,0:T(8,128)(2,1)} %test_hbm.1, bf16[4,3,8,1024]{3,2,1,0:T(8,128)(2,1)} %stored_hbm.1, s32[1]{0:T(128)S(6)} %copy.12.chosen, s32[1,128]{1,0:T(1,128)} %row_hbm.1, ...), custom_call_target="tpu_custom_call" | custom-call | tf_op jit(solution)/shard_map/pallas_call | solution.py:740
  34.1 0.6 %fusion = f32[]{:T(128)} fusion(f32[1,128]{1,0:T(1,128)S(1)} %get-tuple-element.6), kind=kLoop, calls=%fused_computation.1 | loop fusion | flops 383 | bytes 516 | tf_op jit(solution)/shard_map/reduce_sum | solution.py:814
  34.7 0.6 %copy.13 = f32[1,3,8,1024]{3,2,1,0:T(8,128)} copy(f32[1,3,8,1024]{3,2,1,0:T(8,128)S(1)} %get-tuple-element.10) | data formatting | bytes 196608
  35.4 0.5 %copy.14 = f32[1,64]{1,0:T(1,128)} copy(f32[1,64]{1,0:T(1,128)S(1)} %bitcast.1) | data formatting | bytes 512

commit v4 on v3

--- a/solution.py
+++ b/solution.py
@@ -149,9 +149,6 @@
             )
         )
     ]
-    for load in loads[:6]:
-        load.start()
-
     barrier = pltpu.get_barrier_semaphore()
     last_group = groups - 1
 
@@ -179,6 +176,9 @@
         @pl.when(group - offset >= 0)
         def _():
             greet({"tm": group - offset})
+
+    for load in loads[:6]:
+        load.start()
 
     later = jnp.minimum(group, 1)
     greetings = bands - 1 + groups - 1 + (bands - 1) * later

time: 36 us -> 36 us (level)
  no operation moved by 1% of the time
where the time goes in v4:
time: 36 us; the launch traced here: 35.9 us
  Pallas kernels  32.8 us (91%)
  between operations  1.29 us (4%)
  local copies, waits for them, and re-layouts  1.15 us (3%)
  other arithmetic  0.6 us (2%)
    pallas_call x1, Pallas kernels, body(): pl.pallas_call(functools.partial(kernel, groups, bands), out_shape=(jax.S...  32.8 us
    unnamed x2, local copies, waits for them, and re-layouts  1.15 us

profile of v4, /device:TPU:0, one launch (start us, length us, event | category | flops | bytes accessed | tf_op | source)
XLA Modules:
  0.0 35.9 jit_solution(4086728325322178328)
XLA Ops:
  1.3 32.8 %shard_map.94 = (f32[1,3,8,1024]{3,2,1,0:T(8,128)S(1)}, f32[1,128]{1,0:T(1,128)S(1)}) custom-call(bf16[64,3,8,1024]{3,2,1,0:T(8,128)(2,1)} %sketch_hbm.1, bf16[64,3,8,1024]{3,2,1,0:T(8,128)(2,1)} %test_hbm.1, bf16[4,3,8,1024]{3,2,1,0:T(8,128)(2,1)} %stored_hbm.1, s32[1]{0:T(128)S(6)} %copy.12.chosen, s32[1,128]{1,0:T(1,128)} %row_hbm.1, ...), custom_call_target="tpu_custom_call" | custom-call | tf_op jit(solution)/shard_map/pallas_call | solution.py:740
  34.1 0.6 %fusion = f32[]{:T(128)} fusion(f32[1,128]{1,0:T(1,128)S(1)} %get-tuple-element.6), kind=kLoop, calls=%fused_computation.1 | loop fusion | flops 383 | bytes 516 | tf_op jit(solution)/shard_map/reduce_sum | solution.py:814
  34.7 0.6 %copy.13 = f32[1,3,8,1024]{3,2,1,0:T(8,128)} copy(f32[1,3,8,1024]{3,2,1,0:T(8,128)S(1)} %get-tuple-element.10) | data formatting | bytes 196608
  35.4 0.5 %copy.14 = f32[1,64]{1,0:T(1,128)} copy(f32[1,64]{1,0:T(1,128)S(1)} %bitcast.1) | data formatting | bytes 512
